TPU v7x, 8 devices: a whole 2x2x1 slice. The times are simulated.
8 devices in a mesh: model: 8 (over z, y, x, core).
Axes of the slice: x: 2, y: 2, z: 1, core: 2. Of those that a mesh axis runs over, the one named last changes fastest.
Arguments:
- act_in: bfloat16 [2048, 18432], P('model')
- ln_gain: float32 [18432], replicated
- w_q: bfloat16 [18432, 12288], P(None, 'model')
- w_kv: bfloat16 [18432, 512], replicated
- w_o: bfloat16 [12288, 18432], P('model')
- positions: int32 [2048], replicated
Outputs:
- output 1: bfloat16 [2048, 18432], P('model')
- output 2: bfloat16 [2048, 256], replicated
- output 3: bfloat16 [2048, 256], replicated
All inputs are finite; a program needn't handle non-finite values.
Results may differ from a plain program's by a relative error of at most 0.0120546.
Values are sent between devices in bfloat16 or wider.
A program may use at most 1 GiB of HBM per device.

v0:
```python
import jax
import jax.numpy as jnp
from jax import lax
from jax.sharding import PartitionSpec as P

NORM_EPS = 1e-6


def layer_norm(act_rows, gain_vec):
    rows_f32 = act_rows.astype(jnp.float32)
    row_mean = jnp.mean(rows_f32, axis=-1, keepdims=True)
    centered = rows_f32 - row_mean
    variance = jnp.mean(centered * centered, axis=-1, keepdims=True)
    return (centered * lax.rsqrt(variance + NORM_EPS) * gain_vec).astype(jnp.bfloat16)


def attend(q_seqs, k_seqs, v_seqs, positions):
    head_dim = q_seqs.shape[-1]
    scores = jnp.einsum("crie,cle->cril", q_seqs, k_seqs, preferred_element_type=jnp.float32) * head_dim ** -0.5
    visible = positions[None, :] <= positions[:, None]
    scores = jnp.where(visible[None, :, None, :], scores, -1e30)
    attn_prob = jax.nn.softmax(scores, axis=-1).astype(jnp.bfloat16)
    return jnp.einsum("cril,cle->crie", attn_prob, v_seqs, preferred_element_type=jnp.float32).astype(jnp.bfloat16)


def solution(mesh):
    def local_step(x_loc, ln_gain, wq_loc, w_kv, wo_loc, positions):
        seq_len = positions.shape[0]
        head_dim = w_kv.shape[1] // 2
        heads_loc = wq_loc.shape[1] // head_dim
        normed = layer_norm(x_loc, ln_gain)
        kv_loc = jnp.dot(normed, w_kv, preferred_element_type=jnp.float32).astype(jnp.bfloat16)
        normed_all = lax.all_gather(normed, "model", axis=0, tiled=True)
        kv_all = lax.all_gather(kv_loc, "model", axis=0, tiled=True)
        tokens = normed_all.shape[0]
        n_seq = tokens // seq_len
        queries = jnp.dot(normed_all, wq_loc, preferred_element_type=jnp.float32).astype(jnp.bfloat16)
        k_cache = kv_all[:, :head_dim]
        v_cache = kv_all[:, head_dim:]
        attended = attend(queries.reshape(n_seq, seq_len, heads_loc, head_dim), k_cache.reshape(n_seq, seq_len, head_dim), v_cache.reshape(n_seq, seq_len, head_dim), positions)
        y_part = jnp.dot(attended.reshape(tokens, heads_loc * head_dim), wo_loc, preferred_element_type=jnp.float32).astype(jnp.bfloat16)
        y_loc = lax.psum_scatter(y_part, "model", scatter_dimension=0, tiled=True)
        return y_loc, k_cache, v_cache

    return jax.shard_map(
        local_step,
        mesh=mesh,
        in_specs=(P("model", None), P(None), P(None, "model"), P(None, None), P("model", None), P(None)),
        out_specs=(P("model", None), P(None, None), P(None, None)),
        check_vma=False,
    )
```

profile of v0, /device:TPU:0, one launch (start us, length us, event | category | flops | bytes accessed | tf_op | source)
XLA Modules:
  0.0 1160.4 jit_solution(7391580787807219021)
XLA Ops:
  7.2 0.0 copy-start.2
  7.2 0.0 all-gather.5.cloned.1.call-start
  7.2 5.1 convert_reduce_fusion
  12.3 6.3 fusion.8
  18.6 0.0 copy-done.2
  18.6 11.1 fusion.10
  29.7 0.0 copy-start.3
  29.7 12.4 %convolution_convert_fusion.2 = bf16[256,512]{1,0:T(8,128)(2,1)} fusion(bf16[256,18432]{1,0:T(8,128)(2,1)} %fusion.10, bf16[18432,512]{1,0:T(8,128)(2,1)} %param.9), kind=kOutput, calls=%fused_computation.21 | convolution fusion | flops 4831969280 | bytes 28573696 | tf_op jit(solution)/shard_map/dot_general | solution.py:32
  42.1 0.0 all-gather.5.cloned.1.call-update
  42.1 0.0 all-gather.3.cloned.1.call-start
  42.2 0.7 all-gather.3.cloned.1.call-update
  42.9 0.0 reduce-scatter.2.cloned.1.call-start
  42.9 0.0 copy-done.3
  42.9 4.1 broadcast_compare_fusion
  47.0 20.0 %all-gather.5.cloned.1.call-done = bf16[2048,512]{1,0:T(8,128)(2,1)} async-done(((bf16[256,512]{1,0:T(8,128)(2,1)}), bf16[2048,512]{1,0:T(8,128)(2,1)}) %all-gather.5.cloned.1.call-update) | async-done | bytes 2097168 | tf_op jit(solution)/shard_map/all_gather | solution.py:34
  67.0 3.0 fusion.24
  70.0 333.0 %all-gather.3.cloned.1.call-done = bf16[2048,18432]{1,0:T(8,128)(2,1)} async-done(((bf16[256,18432]{1,0:T(8,128)(2,1)}), bf16[2048,18432]{1,0:T(8,128)(2,1)}) %all-gather.3.cloned.1.call-update) | async-done | bytes 75497488 | tf_op jit(solution)/shard_map/all_gather | solution.py:33
  403.0 0.0 copy-start.1
  403.0 128.4 %convolution_convert_fusion.1 = bf16[2048,1536]{0,1:T(8,128)(2,1)} fusion(bf16[2048,18432]{1,0:T(8,128)(2,1)} %all-gather.3.cloned.1.call-done, bf16[18432,1536]{1,0:T(8,128)(2,1)} %param.8), kind=kOutput, calls=%fused_computation.19 | convolution fusion | flops 115967262720 | bytes 138412032 | tf_op jit(solution)/shard_map/dot_general | solution.py:37
  531.5 0.0 copy-done.1
  531.5 0.0 copy-start
  531.5 40.4 %fusion.25 = (f32[2048,6]{0,1:T(8,128)S(1)}, f32[2048,6,2048]{0,2,1:T(8,128)}) fusion(pred[2048,2048]{0,1:T(8,128)(4,1)} %broadcast_compare_fusion, bf16[2048,6,256]{0,2,1:T(8,128)(2,1)} %bitcast.26, bf16[2048,256]{1,0:T(8,128)(2,1)S(1)} %copy-done.1), kind=kOutput, calls=%fused_computation.31 | convolution fusion | flops 12985567232 | bytes 112246784 | tf_op jit(solution)/shard_map/sub | solution.py:22
  571.9 0.0 copy-done
  571.9 38.6 %fusion.13 = bf16[2048,6,256]{0,2,1:T(8,128)(2,1)} fusion(f32[2048,6,2048]{0,2,1:T(8,128)} %get-tuple-element.6, f32[2048,6]{0,1:T(8,128)S(1)} %get-tuple-element.5, bf16[2048,256]{1,0:T(8,128)(2,1)S(1)} %copy-done), kind=kOutput, calls=%fused_computation.20 | convolution fusion | flops 12938379264 | bytes 108052480 | tf_op jit(solution)/shard_map/cril,cle->crie/dot_general | solution.py:23
  610.5 128.0 %convolution_convert_fusion = bf16[2048,18432]{1,0:T(8,128)(2,1)} fusion(bf16[2048,1536]{0,1:T(8,128)(2,1)} %bitcast.27, bf16[1536,18432]{1,0:T(8,128)(2,1)} %param.10), kind=kOutput, calls=%fused_computation.5 | convolution fusion | flops 116001865728 | bytes 138412032 | tf_op jit(solution)/shard_map/dot_general | solution.py:41
  738.5 0.0 reduce-scatter.2.cloned.1.call-update
  738.5 414.9 %reduce-scatter.2.cloned.1.call-done = bf16[256,18432]{1,0:T(8,128)(2,1)} async-done(((bf16[2048,18432]{1,0:T(8,128)(2,1)}), bf16[256,18432]{1,0:T(8,128)(2,1)}) %reduce-scatter.2.cloned.1.call-update) | async-done | bytes 9437200 | tf_op jit(solution)/shard_map/reduce_scatter | solution.py:42
  (2 shorter events, 0.0 us)
Async XLA Ops:
  7.2 11.4 copy-start.2
  7.2 59.9 %all-gather.5.cloned.1.call-start = ((), (), s32[]{:S(2)}) async-start(), calls=%async_computation.2 | async-start | bytes 2359296 | tf_op jit(solution)/shard_map/all_gather | solution.py:34
  29.7 13.2 %copy-start.3 = (s32[2048]{0:T(1024)S(1)}, s32[2048]{0:T(1024)}, u32[]{:S(2)}) copy-start(s32[2048]{0:T(1024)} %param.11) | copy-start | bytes 24580
  42.1 360.9 %all-gather.3.cloned.1.call-start = ((), (), s32[]{:S(2)}) async-start(), calls=%async_computation.1 | async-start | bytes 84934656 | tf_op jit(solution)/shard_map/all_gather | solution.py:33
  42.9 1110.6 %reduce-scatter.2.cloned.1.call-start = ((), (), s32[]{:S(2)}) async-start(), calls=%async_computation.3 | async-start | bytes 84934656 | tf_op jit(solution)/shard_map/reduce_scatter | solution.py:42
  403.0 128.4 %copy-start.1 = (bf16[2048,256]{1,0:T(8,128)(2,1)S(1)}, bf16[2048,256]{1,0:T(8,128)(2,1)}, u32[]{:S(2)}) copy-start(bf16[2048,256]{1,0:T(8,128)(2,1)} %get-tuple-element.4) | copy-start | bytes 3145732
  531.5 40.4 %copy-start = (bf16[2048,256]{1,0:T(8,128)(2,1)S(1)}, bf16[2048,256]{1,0:T(8,128)(2,1)}, u32[]{:S(2)}) copy-start(bf16[2048,256]{1,0:T(8,128)(2,1)} %get-tuple-element.3) | copy-start | bytes 3145732
Sparse Core Ops, SparseCore 0:
  42.2 24.7 all-gather.4
  69.5 333.5 all-gather.2
  738.7 414.7 reduce-scatter.1
where the time goes:
time: 1170 us; the launch traced here: 1160 us
  waiting for transfers between devices  769 us (66%)
  matrix products  348 us (30%)
  other arithmetic  26.6 us (2%)
  between operations  14.2 us (1%)
    reduce_scatter x1, waiting for transfers between devices, local_step(): y_loc = lax.psum_scatter(y_part, 'model', scatter_dimension=0, tiled=True)  415 us
    all_gather x1, waiting for transfers between devices, local_step(): normed_all = lax.all_gather(normed, 'model', axis=0, tiled=True)  333 us
    dot_general x1, matrix products, local_step(): jnp.dot(normed_all, wq_loc, preferred_element_type=jnp.float32)  128 us
    dot_general x1, matrix products, local_step(): jnp.dot(attended.reshape(tokens, heads_loc * head_dim), wo_loc, preferred...  128 us
    sub x1, matrix products, attend(): attn_prob = jax.nn.softmax(scores, axis=-1).astype(jnp.bfloat16)  40.4 us
    dot_general x1, matrix products, attend(): jnp.einsum('cril,cle->crie', attn_prob, v_seqs, preferred_element_type=jn...  38.6 us
  transfers between devices with their start and end apart: 3, of which 3 were waited for; matrix products, arithmetic and copies ran while one was open for 1% of the time, Pallas kernels for 0%

commit v1 on v0

v1 whole, which is shorter than its diff:
```python
import functools

import jax
import jax.numpy as jnp
from jax import lax
from jax.experimental import pallas as pl
from jax.experimental.pallas import tpu as pltpu
from jax.sharding import PartitionSpec as P


NORM_EPS = 1e-6
CORE, XN, YN, DIAG = 1, 2, 4, 6
BF16, F32 = jnp.bfloat16, jnp.float32


def _params(n=1):
    return pltpu.CompilerParams(dimension_semantics=("arbitrary",) * n)


def _norm_kernel(strip, chunk, x_ref, g_ref, *out_refs):
    rows, width = x_ref.shape[-2:]
    n_chunks = width // chunk

    def chunk_of(ref, r, c):
        return ref[0, pl.ds(pl.multiple_of(r * strip, strip), strip), pl.ds(pl.multiple_of(c * chunk, chunk), chunk)]

    def fold(v):
        acc = v[:, :128]
        for i in range(1, chunk // 128):
            acc = acc + v[:, i * 128:(i + 1) * 128]
        return acc

    def one_piece(out_ref):
        def one_strip(r, _):
            def add_sum(c, acc):
                return acc + fold(chunk_of(x_ref, r, c).astype(F32))

            total = lax.fori_loop(0, n_chunks, add_sum, jnp.zeros((strip, 128), F32))
            mean = jnp.sum(total, axis=1, keepdims=True) / width

            def add_sq(c, acc):
                d = chunk_of(x_ref, r, c).astype(F32) - mean
                return acc + fold(d * d)

            sq = lax.fori_loop(0, n_chunks, add_sq, jnp.zeros((strip, 128), F32))
            rstd = lax.rsqrt(jnp.sum(sq, axis=1, keepdims=True) / width + NORM_EPS)

            def put(c, _):
                d = chunk_of(x_ref, r, c).astype(F32) - mean
                cols = pl.ds(pl.multiple_of(c * chunk, chunk), chunk)
                out_ref[pl.ds(pl.multiple_of(r * strip, strip), strip), cols] = (d * rstd * g_ref[:, cols]).astype(BF16)
                return 0

            lax.fori_loop(0, n_chunks, put, 0)
            return 0

        lax.fori_loop(0, rows // strip, one_strip, 0)

    for i, out_ref in enumerate(out_refs):
        pl.when(pl.program_id(0) == i)(functools.partial(one_piece, out_ref))


def norm_pieces(x4, gain, first, step, count):
    _, rows, width = x4.shape
    return pl.pallas_call(
        functools.partial(_norm_kernel, 16, 1024),
        grid=(count,),
        in_specs=[
            pl.BlockSpec((1, rows, width), lambda i: (first + step * i, 0, 0)),
            pl.BlockSpec((1, width), lambda i: (0, 0)),
        ],
        out_specs=[pl.BlockSpec((rows, width), lambda i: (0, 0))] * count,
        out_shape=[jax.ShapeDtypeStruct((rows, width), BF16)] * count,
        compiler_params=_params(),
        cost_estimate=pl.CostEstimate(flops=8 * count * rows * width, bytes_accessed=4 * count * rows * width, transcendentals=0),
        name="norm",
    )(x4, gain)


def _stack_dot_kernel(n_lhs, *refs):
    lhs, (w_ref, out_ref, acc_ref) = refs[:n_lhs], refs[n_lhs:]
    step = pl.program_id(0)
    stacked = jnp.concatenate([r[...] for r in lhs], axis=0)
    part = jnp.dot(stacked, w_ref[...], preferred_element_type=F32)

    @pl.when(step == 0)
    def _():
        acc_ref[...] = part

    @pl.when(step > 0)
    def _():
        acc_ref[...] += part

    @pl.when(step == pl.num_programs(0) - 1)
    def _():
        out_ref[...] = acc_ref[...].astype(BF16)


def stack_dot(lhs, w, depth):
    rows, width = lhs[0].shape
    total, cols = rows * len(lhs), w.shape[1]
    return pl.pallas_call(
        functools.partial(_stack_dot_kernel, len(lhs)),
        grid=(width // depth,),
        in_specs=[pl.BlockSpec((rows, depth), lambda k: (0, k))] * len(lhs) + [pl.BlockSpec((depth, cols), lambda k: (k, 0))],
        out_specs=pl.BlockSpec((total, cols), lambda k: (0, 0)),
        out_shape=jax.ShapeDtypeStruct((total, cols), BF16),
        scratch_shapes=[pltpu.VMEM((total, cols), F32)],
        compiler_params=_params(),
        cost_estimate=pl.CostEstimate(flops=2 * total * width * cols, bytes_accessed=2 * (total * width + width * cols), transcendentals=0),
    )(*lhs, w)


def _unit_kernel(n_lhs, kc, nc, qs, os_, *refs):
    h_refs, (wq, wo, k_hbm, v_hbm, qpos, kpos), refs = refs[:n_lhs], refs[n_lhs:n_lhs + 6], refs[n_lhs + 6:]
    outs, (wq_buf, h_buf, acc, q_buf, o_buf, wo_buf, y_buf, k_buf, v_buf, wq_sem, h_sem, wo_sem, y_sem, kv_sem) = refs[:-14], refs[-14:]
    piece, width = h_refs[0].shape
    _, proj = acc.shape
    head = k_buf.shape[1]
    n_q, n_o = width // kc, wo.shape[1] // nc

    def q_copies(i, slot):
        cols = pl.ds(pl.multiple_of(i * kc, kc), kc)
        cps = [pltpu.make_async_copy(wq.at[cols, :], wq_buf.at[slot], wq_sem.at[slot])]
        for j, h in enumerate(h_refs):
            cps.append(pltpu.make_async_copy(h.at[:, cols], h_buf.at[slot, pl.ds(j * piece, piece), :], h_sem.at[slot, j]))
        return cps

    def o_copy(i, slot):
        return pltpu.make_async_copy(wo.at[:, pl.ds(pl.multiple_of(i * nc, nc), nc)], wo_buf.at[slot], wo_sem.at[slot])

    def y_copies(i, slot):
        cols = pl.ds(pl.multiple_of(i * nc, nc), nc)
        cps, at = [], 0
        for j, out in enumerate(outs):
            n = out.shape[0]
            cps.append(pltpu.make_async_copy(y_buf.at[slot, pl.ds(at, n), :], out.at[:, cols], y_sem.at[slot, j]))
            at += n
        return cps

    for i in range(qs):
        for c in q_copies(i, i):
            c.start()
    kv = [pltpu.make_async_copy(k_hbm, k_buf, kv_sem.at[0]), pltpu.make_async_copy(v_hbm, v_buf, kv_sem.at[1])]
    for c in kv:
        c.start()
    acc[...] = jnp.zeros_like(acc)

    def q_step(i, _):
        slot = lax.rem(i, qs)
        for c in q_copies(i, slot):
            c.wait()
        acc[...] += jnp.dot(h_buf[slot], wq_buf[slot], preferred_element_type=F32)

        @pl.when(i + qs < n_q)
        def _():
            for c in q_copies(i + qs, slot):
                c.start()

        return 0

    lax.fori_loop(0, n_q, q_step, 0)
    for i in range(os_):
        o_copy(i, i).start()
    q_buf[...] = acc[...].astype(BF16)
    for c in kv:
        c.wait()

    def one_head(n, _):
        cols = pl.ds(pl.multiple_of(n * head, head), head)
        s = lax.dot_general(q_buf[:, cols], k_buf[...], (((1,), (1,)), ((), ())), preferred_element_type=F32)
        s = jnp.where(kpos[...] <= qpos[...], s, -1e30)
        top = jnp.max(s, axis=-1, keepdims=True)
        e = jnp.exp((s - top) * (head ** -0.5))
        p = (e * (1.0 / jnp.sum(e, axis=-1, keepdims=True))).astype(BF16)
        o_buf[:, cols] = jnp.dot(p, v_buf[...], preferred_element_type=F32).astype(BF16)
        return 0

    lax.fori_loop(0, proj // head, one_head, 0)


    def o_step(i, _):
        slot, yslot = lax.rem(i, os_), lax.rem(i, 2)
        o_copy(i, slot).wait()

        @pl.when(i >= 2)
        def _():
            for c in y_copies(i - 2, yslot):
                c.wait()

        y_buf[yslot] = jnp.dot(o_buf[...], wo_buf[slot], preferred_element_type=F32).astype(BF16)
        for c in y_copies(i, yslot):
            c.start()

        @pl.when(i + os_ < n_o)
        def _():
            o_copy(i + os_, slot).start()

        return 0

    lax.fori_loop(0, n_o, o_step, 0)
    for i in (n_o - 2, n_o - 1):
        for c in y_copies(i, i % 2):
            c.wait()


def unit_call(hs, wq, wo, k, v, qpos, kpos, index, splits, kc=1024, nc=1024, qs=4, os_=3):
    piece, width = hs[0].shape
    n = len(hs)
    rows = piece * n
    proj = wq.shape[1]
    keys, head = k.shape
    any_ = pl.BlockSpec(memory_space=pl.ANY)
    heads = proj // head
    return pl.pallas_call(
        functools.partial(_unit_kernel, n, kc, nc, qs, os_),
        grid=(1,),
        in_specs=[any_] * (n + 4) + [pl.BlockSpec((rows, 1), lambda i: (index, 0)), pl.BlockSpec((1, keys), lambda i: (0, 0))],
        out_specs=[any_] * len(splits),
        out_shape=[jax.ShapeDtypeStruct((r, width), BF16) for r in splits],
        scratch_shapes=[
            pltpu.VMEM((qs, kc, proj), BF16), pltpu.VMEM((qs, rows, kc), BF16), pltpu.VMEM((rows, proj), F32),
            pltpu.VMEM((rows, proj), BF16), pltpu.VMEM((rows, proj), BF16), pltpu.VMEM((os_, proj, nc), BF16),
            pltpu.VMEM((2, rows, nc), BF16), pltpu.VMEM((keys, head), BF16), pltpu.VMEM((keys, head), BF16),
            pltpu.SemaphoreType.DMA((qs,)), pltpu.SemaphoreType.DMA((qs, n)), pltpu.SemaphoreType.DMA((os_,)),
            pltpu.SemaphoreType.DMA((2, len(splits))), pltpu.SemaphoreType.DMA((2,)),
        ],
        compiler_params=pltpu.CompilerParams(dimension_semantics=("arbitrary",)),
        cost_estimate=pl.CostEstimate(flops=2 * rows * proj * (2 * width + 2 * keys), bytes_accessed=2 * (2 * width * proj + 2 * rows * width), transcendentals=rows * keys * heads),
        name="unit",
    )(*hs, wq, wo, k, v, qpos, kpos)


def add(*terms):
    total = terms[0].astype(F32)
    for t in terms[1:]:
        total = total + t.astype(F32)
    return total.astype(BF16)


UNITS = ("u1a", "u1b", "u2a", "u2b", "u3a", "u3b", "u0a", "u0b")


def solution(mesh):
    n_dev = mesh.shape["model"]

    def send(value, mask):
        return lax.ppermute(value, "model", [(i, i ^ mask) for i in range(n_dev)])

    def by_mask(arr, me):
        cube = arr.reshape((2, 2, 2) + arr.shape[1:])
        for axis, bit in ((0, 4), (1, 2), (2, 1)):
            cube = jnp.where((me & bit) != 0, jnp.flip(cube, axis), cube)
        return cube.reshape(arr.shape)

    def local_step(x_loc, ln_gain, wq_loc, w_kv, wo_loc, positions):
        me = lax.axis_index("model")
        rows, width = x_loc.shape
        head = w_kv.shape[1] // 2
        seq = positions.shape[0]
        piece = rows // 4
        x4 = x_loc.reshape(4, piece, width)
        gain = ln_gain.reshape(1, width)

        h, fx, fy, fd = [None] * 4, [None] * 4, [None] * 4, [None] * 4
        h[0], h[2] = norm_pieces(x4, gain, 0, 2, 2)
        fx[0], fy[2] = send(h[0], XN), send(h[2], YN)
        h[1], h[3] = norm_pieces(x4, gain, 1, 2, 2)
        kv = stack_dot(h, w_kv, 2048)
        kv_m = [kv] + [None] * 7
        for m in (XN, YN, DIAG):
            kv_m[m] = send(kv, m)
        fx[1], fy[3] = send(h[1], XN), send(h[3], YN)
        fx[2], fy[0] = send(h[2], XN), send(h[0], YN)
        fx[3], fy[1] = send(h[3], XN), send(h[1], YN)
        fd[0], fd[2] = send(fx[0], YN), send(fy[2], XN)
        fd[1], fd[3] = send(fx[1], YN), send(fy[3], XN)
        for m in (0, XN, YN, DIAG):
            kv_m[m | CORE] = send(kv_m[m], CORE)

        kv_all = by_mask(jnp.stack(kv_m), me).reshape(seq, 2 * head)
        k_cache, v_cache = kv_all[:, :head], kv_all[:, head:]
        pos_m = by_mask(positions.reshape(n_dev, 4, piece), me)
        kpos = positions.reshape(1, seq)
        plan = {
            "u0a": ((0, 0, h[0]), (0, 2, h[2])), "u0b": ((0, 1, h[1]), (0, 3, h[3])),
            "u1a": ((XN, 0, fx[0]), (YN, 2, fy[2])), "u1b": ((XN, 1, fx[1]), (YN, 3, fy[3])),
            "u2a": ((XN, 2, fx[2]), (YN, 0, fy[0])), "u2b": ((XN, 3, fx[3]), (YN, 1, fy[1])),
            "u3a": ((DIAG, 0, fd[0]), (DIAG, 2, fd[2])), "u3b": ((DIAG, 1, fd[1]), (DIAG, 3, fd[3])),
        }
        qpos = jnp.concatenate([pos_m[m | c, i] for u in UNITS for c in (0, CORE) for m, i, _ in plan[u]]).reshape(-1, 1)

        def unit(name):
            mine = [b[2] for b in plan[name]]
            swapped = [send(b, CORE) for b in mine]
            ya, yb, other = unit_call(mine + swapped, wq_loc, wo_loc, k_cache, v_cache, qpos, kpos, UNITS.index(name), [piece, piece, 2 * piece])
            back = send(other, CORE)
            return (ya, back[:piece]), (yb, back[piece:])

        x0, y2 = unit("u1a")
        x1, y3 = unit("u1b")
        x2, y0 = unit("u2a")
        x3, y1 = unit("u2b")
        d0, d2 = unit("u3a")
        d1, d3 = unit("u3b")
        o0, o2 = unit("u0a")
        o1, o3 = unit("u0b")

        rx0, ry2 = send(add(*x0), XN), send(add(*y2), YN)
        rx1, ry3 = send(add(*x1), XN), send(add(*y3), YN)
        hx0, hy2 = send(add(*d0), XN), send(add(*d2), YN)
        hx1, hy3 = send(add(*d1), XN), send(add(*d3), YN)
        ry0, rx2 = send(add(*y0, hx0), YN), send(add(*x2, hy2), XN)
        ry1, rx3 = send(add(*y1, hx1), YN), send(add(*x3, hy3), XN)
        y_loc = jnp.concatenate([add(*o0, rx0, ry0), add(*o1, rx1, ry1), add(*o2, rx2, ry2), add(*o3, rx3, ry3)], axis=0)
        return y_loc, k_cache, v_cache

    return jax.shard_map(
        local_step,
        mesh=mesh,
        in_specs=(P("model", None), P(None), P(None, "model"), P(None, None), P("model", None), P(None)),
        out_specs=(P("model", None), P(None, None), P(None, None)),
        check_vma=False,
    )
```

time: 1170 us -> 884 us (0.76)
  Pallas kernels: 0 us -> 475 us
  waiting for transfers between devices: 769 us -> 312 us
  matrix products: 348 us -> 0 us
  starting transfers between devices: 0.12 us -> 35 us
  other arithmetic: 26.6 us -> 43.5 us
  between operations: 14.2 us -> 1.3 us
    pallas_call x0 -> x11, Pallas kernels: none -> 475 us  [the longest x8 437 us: unit_call(): pl.pallas_call(functools.partial(_unit_kernel, n, kc, nc, qs, os_), grid=...]
    reduce_scatter x1 -> x0, waiting for transfers between devices: 415 us -> none  [local_step(): y_loc = lax.psum_scatter(y_part, 'model', scatter_dimension=0, tiled=True)]
    all_gather x2 -> x0, waiting for transfers between devices: 353 us -> none  [the longest x1 333 us: local_step(): normed_all = lax.all_gather(normed, 'model', axis=0, tiled=True)]
    ppermute x0 -> x55, waiting for transfers between devices: none -> 312 us  [send(): return lax.ppermute(value, 'model', [(i, i ^ mask) for i in range(n_dev)])]
    dot_general x4 -> x0, matrix products: 307 us -> none  [the longest x1 128 us: local_step(): jnp.dot(normed_all, wq_loc, preferred_element_type=jnp.float32)]
    sub x1 -> x0, matrix products: 40.4 us -> none  [attend(): attn_prob = jax.nn.softmax(scores, axis=-1).astype(jnp.bfloat16)]
    ppermute x0 -> x55, starting transfers between devices: none -> 35 us  [send(): return lax.ppermute(value, 'model', [(i, i ^ mask) for i in range(n_dev)])]
    convert_element_type x1 -> x8, other arithmetic: 11.1 us -> 37.7 us  [add(): return total.astype(BF16)]
  transfers between devices with their start and end apart: 3 -> 55, of which waited for: 3 -> 11; matrix products, arithmetic and copies ran while one was open for 1% -> 4% of each run, Pallas kernels for 0% -> 53%
where the time goes in v1:
time: 884 us; the launch traced here: 875 us
  Pallas kernels  475 us (54%)
  waiting for transfers between devices  312 us (35%)
  other arithmetic  43.5 us (5%)
  starting transfers between devices  35 us (4%)
    pallas_call x8, Pallas kernels, unit_call(): pl.pallas_call(functools.partial(_unit_kernel, n, kc, nc, qs, os_), grid=...  437 us
    ppermute x55, waiting for transfers between devices, send(): return lax.ppermute(value, 'model', [(i, i ^ mask) for i in range(n_dev)])  312 us
    convert_element_type x8, other arithmetic, add(): return total.astype(BF16)  37.7 us
    ppermute x55, starting transfers between devices, send(): return lax.ppermute(value, 'model', [(i, i ^ mask) for i in range(n_dev)])  35 us
    pallas_call x2, Pallas kernels, norm_pieces(): pl.pallas_call(functools.partial(_norm_kernel, 16, 1024), grid=(count,),...  23.4 us
  transfers between devices with their start and end apart: 55, of which 11 were waited for; matrix products, arithmetic and copies ran while one was open for 4% of the time, Pallas kernels for 53%

profile of v1, /device:TPU:0, one launch (start us, length us, event | category | flops | bytes accessed | tf_op | source)
XLA Modules:
  0.0 875.0 jit_solution(4062244726129975865)
XLA Ops:
  0.6 11.8 %norm.3 = (bf16[64,18432]{1,0:T(8,128)(2,1)}, bf16[64,18432]{1,0:T(8,128)(2,1)}) custom-call(bf16[4,64,18432]{2,1,0:T(8,128)(2,1)} %bitcast.87, f32[1,18432]{1,0:T(1,128)} %bitcast.99), custom_call_target="tpu_custom_call" | custom-call | flops 18874368 | bytes 9437184 | tf_op jit(solution)/shard_map/norm/pallas_call | solution.py:65
  12.4 3.3 collective-permute-start.31
  15.7 11.6 %norm.2 = (bf16[64,18432]{1,0:T(8,128)(2,1)}, bf16[64,18432]{1,0:T(8,128)(2,1)}) custom-call(bf16[4,64,18432]{2,1,0:T(8,128)(2,1)} %bitcast.88, f32[1,18432]{1,0:T(1,128)} %bitcast.100), custom_call_target="tpu_custom_call" | custom-call | flops 18874368 | bytes 9437184 | tf_op jit(solution)/shard_map/norm/pallas_call | solution.py:65
  27.4 14.6 %shard_map.85 = bf16[256,512]{1,0:T(8,128)(2,1)} custom-call(bf16[64,18432]{1,0:T(8,128)(2,1)} %get-tuple-element.31.refs_0_, bf16[64,18432]{1,0:T(8,128)(2,1)} %get-tuple-element.33.refs_1_.refs_0_, bf16[64,18432]{1,0:T(8,128)(2,1)} %get-tuple-element.32.refs_2_.refs_1_, bf16[64,18432]{1,0:T(8,128)(2,1)} %get-tuple-element.34.refs_3_.refs_1_, ...), custom_call_target="tpu_custom_call" | custom-call | flops 4831838208 | bytes 28311552 | tf_op jit(solution)/shard_map/pallas_call | solution.py:102
  42.0 2.0 collective-permute-start.5
  44.1 1.4 collective-permute-start.7
  45.7 1.4 copy.9.refs_8_
  47.1 1.0 bitcast_dynamic-update-slice_fusion.7
  48.1 25.5 %collective-permute-done.3 = bf16[256,512]{1,0:T(8,128)(2,1)S(1)} collective-permute-done((bf16[256,512]{1,0:T(8,128)(2,1)}, bf16[256,512]{1,0:T(8,128)(2,1)S(1)}, u32[]{:S(2)}, u32[]{:S(2)}) %collective-permute-start.3) | collective-permute-done | bytes 262176 | tf_op jit(solution)/shard_map/ppermute | solution.py:248
  75.4 4.3 collective-permute-done.7
  79.6 1.5 collective-permute-start.37
  81.2 1.5 collective-permute-done.8
  84.6 1.5 fusion
  86.0 1.4 copy-done.20
  88.0 54.5 %unit.12 = (bf16[64,18432]{1,0:T(8,128)(2,1)}, bf16[64,18432]{1,0:T(8,128)(2,1)}, bf16[128,18432]{1,0:T(8,128)(2,1)}) custom-call(bf16[64,18432]{1,0:T(8,128)(2,1)} %get-tuple-element.33.refs_1_.refs_0_, bf16[64,18432]{1,0:T(8,128)(2,1)} %get-tuple-element.34.refs_3_.refs_1_, bf16[64,18432]{1,0:T(8,128)(2,1)} %copy-done.20, ...), custom_call_target="tpu_custom_call" | custom-call | flops 32212254720 | bytes 132120576 | tf_op jit(solution)/shard_map/unit/pallas_call | solution.py:215
  142.5 1.5 collective-permute-start.32
  145.1 54.5 %unit.8 = (bf16[64,18432]{1,0:T(8,128)(2,1)}, bf16[64,18432]{1,0:T(8,128)(2,1)}, bf16[128,18432]{1,0:T(8,128)(2,1)}) custom-call(bf16[64,18432]{1,0:T(8,128)(2,1)} %get-tuple-element.31.refs_0_, bf16[64,18432]{1,0:T(8,128)(2,1)} %get-tuple-element.32.refs_2_.refs_1_, bf16[64,18432]{1,0:T(8,128)(2,1)} %collective-permute-done.refs_2_, ...), custom_call_target="tpu_custom_call" | custom-call | flops 32212254720 | bytes 132120576 | tf_op jit(solution)/shard_map/unit/pallas_call | solution.py:215
  199.6 1.5 collective-permute-start.16
  202.2 55.0 %unit.14 = (bf16[64,18432]{1,0:T(8,128)(2,1)}, bf16[64,18432]{1,0:T(8,128)(2,1)}, bf16[128,18432]{1,0:T(8,128)(2,1)}) custom-call(bf16[64,18432]{1,0:T(8,128)(2,1)} %collective-permute-done.37.refs_0_, bf16[64,18432]{1,0:T(8,128)(2,1)} %collective-permute-done.38.refs_1_, bf16[64,18432]{1,0:T(8,128)(2,1)} %collective-permute-done.39.refs_2_, ...), custom_call_target="tpu_custom_call" | custom-call | flops 32212254720 | bytes 132120576 | tf_op jit(solution)/shard_map/unit/pallas_call | solution.py:215
  257.2 1.5 collective-permute-start.11
  259.3 54.5 %unit.13 = (bf16[64,18432]{1,0:T(8,128)(2,1)}, bf16[64,18432]{1,0:T(8,128)(2,1)}, bf16[128,18432]{1,0:T(8,128)(2,1)}) custom-call(bf16[64,18432]{1,0:T(8,128)(2,1)} %collective-permute-done.31.refs_0_, bf16[64,18432]{1,0:T(8,128)(2,1)} %collective-permute-done.32.refs_1_, bf16[64,18432]{1,0:T(8,128)(2,1)} %collective-permute-done.33.refs_2_, ...), custom_call_target="tpu_custom_call" | custom-call | flops 32212254720 | bytes 132120576 | tf_op jit(solution)/shard_map/unit/pallas_call | solution.py:215
  315.8 54.6 %unit.10 = (bf16[64,18432]{1,0:T(8,128)(2,1)}, bf16[64,18432]{1,0:T(8,128)(2,1)}, bf16[128,18432]{1,0:T(8,128)(2,1)}) custom-call(bf16[64,18432]{1,0:T(8,128)(2,1)} %collective-permute-done.16.refs_0_, bf16[64,18432]{1,0:T(8,128)(2,1)} %collective-permute-done.17.refs_1_, bf16[64,18432]{1,0:T(8,128)(2,1)} %collective-permute-done.18.refs_2_, ...), custom_call_target="tpu_custom_call" | custom-call | flops 32212254720 | bytes 132120576 | tf_op jit(solution)/shard_map/unit/pallas_call | solution.py:215
  370.4 1.2 collective-permute-start.21
  371.5 1.5 collective-permute-start.22
  373.5 54.5 %unit.9 = (bf16[64,18432]{1,0:T(8,128)(2,1)}, bf16[64,18432]{1,0:T(8,128)(2,1)}, bf16[128,18432]{1,0:T(8,128)(2,1)}) custom-call(bf16[64,18432]{1,0:T(8,128)(2,1)} %copy-done.19, bf16[64,18432]{1,0:T(8,128)(2,1)} %collective-permute-done.11.refs_1_, bf16[64,18432]{1,0:T(8,128)(2,1)} %collective-permute-done.12.refs_2_, ...), custom_call_target="tpu_custom_call" | custom-call | flops 32212254720 | bytes 132120576 | tf_op jit(solution)/shard_map/unit/pallas_call | solution.py:215
  429.1 54.6 %unit.15 = (bf16[64,18432]{1,0:T(8,128)(2,1)}, bf16[64,18432]{1,0:T(8,128)(2,1)}, bf16[128,18432]{1,0:T(8,128)(2,1)}) custom-call(bf16[64,18432]{1,0:T(8,128)(2,1)} %collective-permute-done.42.refs_0_, bf16[64,18432]{1,0:T(8,128)(2,1)} %collective-permute-done.43.refs_1_, bf16[64,18432]{1,0:T(8,128)(2,1)} %collective-permute-done.44.refs_2_, ...), custom_call_target="tpu_custom_call" | custom-call | flops 32212254720 | bytes 132120576 | tf_op jit(solution)/shard_map/unit/pallas_call | solution.py:215
  483.9 1.4 copy-done.21
  485.3 54.7 %unit.11 = (bf16[64,18432]{1,0:T(8,128)(2,1)}, bf16[64,18432]{1,0:T(8,128)(2,1)}, bf16[128,18432]{1,0:T(8,128)(2,1)}) custom-call(bf16[64,18432]{1,0:T(8,128)(2,1)} %collective-permute-done.21.refs_0_, bf16[64,18432]{1,0:T(8,128)(2,1)} %collective-permute-done.22.refs_1_, bf16[64,18432]{1,0:T(8,128)(2,1)} %copy-done.21, ...), custom_call_target="tpu_custom_call" | custom-call | flops 32212254720 | bytes 132120576 | tf_op jit(solution)/shard_map/unit/pallas_call | solution.py:215
  540.5 6.5 add_convert_fusion.11
  547.1 5.9 add_convert_fusion.15
  553.0 3.6 add_convert_fusion.10
  558.0 3.5 add_convert_fusion.14
  561.6 48.9 %collective-permute-done.47 = bf16[64,18432]{1,0:T(8,128)(2,1)S(1)} collective-permute-done((bf16[64,18432]{1,0:T(8,128)(2,1)}, bf16[64,18432]{1,0:T(8,128)(2,1)S(1)}, u32[]{:S(2)}, u32[]{:S(2)}) %collective-permute-start.47) | collective-permute-done | bytes 2359328 | tf_op jit(solution)/shard_map/ppermute | solution.py:248
  611.9 3.5 add_convert_fusion.9
  615.4 1.1 collective-permute-start.36
  616.5 1.5 collective-permute-start.54
  618.1 46.7 %collective-permute-done.26 = bf16[64,18432]{1,0:T(8,128)(2,1)S(1)} collective-permute-done((bf16[64,18432]{1,0:T(8,128)(2,1)}, bf16[64,18432]{1,0:T(8,128)(2,1)S(1)}, u32[]{:S(2)}, u32[]{:S(2)}) %collective-permute-start.26) | collective-permute-done | bytes 2359328 | tf_op jit(solution)/shard_map/ppermute | solution.py:248
  665.3 1.4 copy-done.11
  666.7 1.5 collective-permute-start.53
  668.2 5.3 add_convert_fusion.13
  673.6 41.8 %collective-permute-done.36 = bf16[64,18432]{1,0:T(8,128)(2,1)S(1)} collective-permute-done((bf16[64,18432]{1,0:T(8,128)(2,1)}, bf16[64,18432]{1,0:T(8,128)(2,1)S(1)}, u32[]{:S(2)}, u32[]{:S(2)}) %collective-permute-start.36) | collective-permute-done | bytes 2359328 | tf_op jit(solution)/shard_map/ppermute | solution.py:248
  716.8 49.7 %collective-permute-done.48 = bf16[64,18432]{1,0:T(8,128)(2,1)S(1)} collective-permute-done((bf16[64,18432]{1,0:T(8,128)(2,1)S(1)}, bf16[64,18432]{1,0:T(8,128)(2,1)S(1)}, u32[]{:S(2)}, u32[]{:S(2)}) %collective-permute-start.48) | collective-permute-done | bytes 2359328 | tf_op jit(solution)/shard_map/ppermute | solution.py:248
  767.3 1.1 collective-permute-start.50
  768.8 5.1 add_convert_fusion.8
  773.8 42.6 %collective-permute-done.15 = bf16[64,18432]{1,0:T(8,128)(2,1)S(1)} collective-permute-done((bf16[64,18432]{1,0:T(8,128)(2,1)}, bf16[64,18432]{1,0:T(8,128)(2,1)S(1)}, u32[]{:S(2)}, u32[]{:S(2)}) %collective-permute-start.15) | collective-permute-done | bytes 2359328 | tf_op jit(solution)/shard_map/ppermute | solution.py:248
  817.1 48.9 %collective-permute-done.27 = bf16[64,18432]{1,0:T(8,128)(2,1)} collective-permute-done((bf16[64,18432]{1,0:T(8,128)(2,1)}, bf16[64,18432]{1,0:T(8,128)(2,1)}, u32[]{:S(2)}, u32[]{:S(2)}) %collective-permute-start.27) | collective-permute-done | bytes 2359328 | tf_op jit(solution)/shard_map/ppermute | solution.py:248
  866.0 4.3 add_convert_fusion.12
  870.4 4.4 pad_maximum_fusion
  (148 shorter events, 17.9 us)
Async XLA Ops:
  12.4 187.2 %collective-permute-start.31 = (bf16[64,18432]{1,0:T(8,128)(2,1)}, bf16[64,18432]{1,0:T(8,128)(2,1)}, u32[]{:S(2)}, u32[]{:S(2)}) collective-permute-start(bf16[64,18432]{1,0:T(8,128)(2,1)} %get-tuple-element.33.refs_1_.refs_0_), channel_id=1, source_target_pairs={{0,2},{1,3},{2,0},{3,1},{4,6},{5,7},{6,4},{7,5}} | collective-permute-start | bytes 7077896 | tf_op jit(solution)/shard_map/ppermute | solution.py:248
  42.0 31.6 %collective-permute-start.3 = (bf16[256,512]{1,0:T(8,128)(2,1)}, bf16[256,512]{1,0:T(8,128)(2,1)S(1)}, u32[]{:S(2)}, u32[]{:S(2)}) collective-permute-start(bf16[256,512]{1,0:T(8,128)(2,1)} %shard_map.85), channel_id=1, source_target_pairs={{0,2},{1,3},{2,0},{3,1},{4,6},{5,7},{6,4},{7,5}} | collective-permute-start | bytes 786440 | tf_op jit(solution)/shard_map/ppermute | solution.py:248
  42.0 31.7 %collective-permute-start.5 = (bf16[256,512]{1,0:T(8,128)(2,1)}, bf16[256,512]{1,0:T(8,128)(2,1)S(1)}, u32[]{:S(2)}, u32[]{:S(2)}) collective-permute-start(bf16[256,512]{1,0:T(8,128)(2,1)} %shard_map.85), channel_id=1, source_target_pairs={{0,4},{1,5},{2,6},{3,7},{4,0},{5,1},{6,2},{7,3}} | collective-permute-start | bytes 786440 | tf_op jit(solution)/shard_map/ppermute | solution.py:248
  44.1 35.6 %collective-permute-start.7 = (bf16[256,512]{1,0:T(8,128)(2,1)}, bf16[256,512]{1,0:T(8,128)(2,1)S(1)}, u32[]{:S(2)}, u32[]{:S(2)}) collective-permute-start(bf16[256,512]{1,0:T(8,128)(2,1)} %shard_map.85), channel_id=1, source_target_pairs={{0,6},{1,7},{2,4},{3,5},{4,2},{5,3},{6,0},{7,1}} | collective-permute-start | bytes 786440 | tf_op jit(solution)/shard_map/ppermute | solution.py:248
  48.1 37.9 %collective-permute-start.28 = (bf16[64,18432]{1,0:T(8,128)(2,1)S(1)}, bf16[64,18432]{1,0:T(8,128)(2,1)S(1)}, u32[]{:S(2)}, u32[]{:S(2)}) collective-permute-start(bf16[64,18432]{1,0:T(8,128)(2,1)S(1)} %copy-done), channel_id=1, source_target_pairs={{0,1},{1,0},{2,3},{3,2},{4,5},{5,4},{6,7},{7,6}} | collective-permute-start | bytes 7077896 | tf_op jit(solution)/shard_map/ppermute | solution.py:248
  79.6 62.9 %collective-permute-start.37 = (bf16[64,18432]{1,0:T(8,128)(2,1)}, bf16[64,18432]{1,0:T(8,128)(2,1)}, u32[]{:S(2)}, u32[]{:S(2)}) collective-permute-start(bf16[64,18432]{1,0:T(8,128)(2,1)} %get-tuple-element.34.refs_3_.refs_1_), channel_id=1, source_target_pairs={{0,2},{1,3},{2,0},{3,1},{4,6},{5,7},{6,4},{7,5}} | collective-permute-start | bytes 7077896 | tf_op jit(solution)/shard_map/ppermute | solution.py:248
  82.7 61.4 %collective-permute-start.38 = (bf16[64,18432]{1,0:T(8,128)(2,1)S(1)}, bf16[64,18432]{1,0:T(8,128)(2,1)}, u32[]{:S(2)}, u32[]{:S(2)}) collective-permute-start(bf16[64,18432]{1,0:T(8,128)(2,1)S(1)} %copy-done), channel_id=1, source_target_pairs={{0,4},{1,5},{2,6},{3,7},{4,0},{5,1},{6,2},{7,3}} | collective-permute-start | bytes 7077896 | tf_op jit(solution)/shard_map/ppermute | solution.py:248
  87.4 57.1 %collective-permute-start = (bf16[64,18432]{1,0:T(8,128)(2,1)}, bf16[64,18432]{1,0:T(8,128)(2,1)}, u32[]{:S(2)}, u32[]{:S(2)}) collective-permute-start(bf16[64,18432]{1,0:T(8,128)(2,1)} %get-tuple-element.31.refs_0_), channel_id=1, source_target_pairs={{0,1},{1,0},{2,3},{3,2},{4,5},{5,4},{6,7},{7,6}} | collective-permute-start | bytes 7077896 | tf_op jit(solution)/shard_map/ppermute | solution.py:248
  87.5 57.1 %collective-permute-start.1 = (bf16[64,18432]{1,0:T(8,128)(2,1)}, bf16[64,18432]{1,0:T(8,128)(2,1)}, u32[]{:S(2)}, u32[]{:S(2)}) collective-permute-start(bf16[64,18432]{1,0:T(8,128)(2,1)} %get-tuple-element.32.refs_2_.refs_1_), channel_id=1, source_target_pairs={{0,1},{1,0},{2,3},{3,2},{4,5},{5,4},{6,7},{7,6}} | collective-permute-start | bytes 7077896 | tf_op jit(solution)/shard_map/ppermute | solution.py:248
  142.5 58.7 %collective-permute-start.32 = (bf16[64,18432]{1,0:T(8,128)(2,1)}, bf16[64,18432]{1,0:T(8,128)(2,1)}, u32[]{:S(2)}, u32[]{:S(2)}) collective-permute-start(bf16[64,18432]{1,0:T(8,128)(2,1)} %get-tuple-element.34.refs_3_.refs_1_), channel_id=1, source_target_pairs={{0,4},{1,5},{2,6},{3,7},{4,0},{5,1},{6,2},{7,3}} | collective-permute-start | bytes 7077896 | tf_op jit(solution)/shard_map/ppermute | solution.py:248
  144.1 169.7 %collective-permute-start.10 = (bf16[64,18432]{1,0:T(8,128)(2,1)}, bf16[64,18432]{1,0:T(8,128)(2,1)S(1)}, u32[]{:S(2)}, u32[]{:S(2)}) collective-permute-start(bf16[64,18432]{1,0:T(8,128)(2,1)} %get-tuple-element.31.refs_0_), channel_id=1, source_target_pairs={{0,2},{1,3},{2,0},{3,1},{4,6},{5,7},{6,4},{7,5}} | collective-permute-start | bytes 7077896 | tf_op jit(solution)/shard_map/ppermute | solution.py:248
  144.6 57.1 %collective-permute-start.39 = (bf16[64,18432]{1,0:T(8,128)(2,1)}, bf16[64,18432]{1,0:T(8,128)(2,1)}, u32[]{:S(2)}, u32[]{:S(2)}) collective-permute-start(bf16[64,18432]{1,0:T(8,128)(2,1)} %collective-permute-done.37.refs_0_), channel_id=1, source_target_pairs={{0,1},{1,0},{2,3},{3,2},{4,5},{5,4},{6,7},{7,6}} | collective-permute-start | bytes 7077896 | tf_op jit(solution)/shard_map/ppermute | solution.py:248
  144.6 57.1 %collective-permute-start.40 = (bf16[64,18432]{1,0:T(8,128)(2,1)}, bf16[64,18432]{1,0:T(8,128)(2,1)}, u32[]{:S(2)}, u32[]{:S(2)}) collective-permute-start(bf16[64,18432]{1,0:T(8,128)(2,1)} %collective-permute-done.38.refs_1_), channel_id=1, source_target_pairs={{0,1},{1,0},{2,3},{3,2},{4,5},{5,4},{6,7},{7,6}} | collective-permute-start | bytes 7077896 | tf_op jit(solution)/shard_map/ppermute | solution.py:248
  199.6 57.5 %collective-permute-start.16 = (bf16[64,18432]{1,0:T(8,128)(2,1)}, bf16[64,18432]{1,0:T(8,128)(2,1)}, u32[]{:S(2)}, u32[]{:S(2)}) collective-permute-start(bf16[64,18432]{1,0:T(8,128)(2,1)} %get-tuple-element.32.refs_2_.refs_1_), channel_id=1, source_target_pairs={{0,2},{1,3},{2,0},{3,1},{4,6},{5,7},{6,4},{7,5}} | collective-permute-start | bytes 7077896 | tf_op jit(solution)/shard_map/ppermute | solution.py:248
  201.2 57.6 %collective-permute-start.17 = (bf16[64,18432]{1,0:T(8,128)(2,1)}, bf16[64,18432]{1,0:T(8,128)(2,1)}, u32[]{:S(2)}, u32[]{:S(2)}) collective-permute-start(bf16[64,18432]{1,0:T(8,128)(2,1)} %get-tuple-element.31.refs_0_), channel_id=1, source_target_pairs={{0,4},{1,5},{2,6},{3,7},{4,0},{5,1},{6,2},{7,3}} | collective-permute-start | bytes 7077896 | tf_op jit(solution)/shard_map/ppermute | solution.py:248
  201.7 57.1 %collective-permute-start.33 = (bf16[64,18432]{1,0:T(8,128)(2,1)}, bf16[64,18432]{1,0:T(8,128)(2,1)}, u32[]{:S(2)}, u32[]{:S(2)}) collective-permute-start(bf16[64,18432]{1,0:T(8,128)(2,1)} %collective-permute-done.31.refs_0_), channel_id=1, source_target_pairs={{0,1},{1,0},{2,3},{3,2},{4,5},{5,4},{6,7},{7,6}} | collective-permute-start | bytes 7077896 | tf_op jit(solution)/shard_map/ppermute | solution.py:248
  201.7 57.6 %collective-permute-start.34 = (bf16[64,18432]{1,0:T(8,128)(2,1)}, bf16[64,18432]{1,0:T(8,128)(2,1)}, u32[]{:S(2)}, u32[]{:S(2)}) collective-permute-start(bf16[64,18432]{1,0:T(8,128)(2,1)} %collective-permute-done.32.refs_1_), channel_id=1, source_target_pairs={{0,1},{1,0},{2,3},{3,2},{4,5},{5,4},{6,7},{7,6}} | collective-permute-start | bytes 7077896 | tf_op jit(solution)/shard_map/ppermute | solution.py:248
  257.2 57.2 %collective-permute-start.11 = (bf16[64,18432]{1,0:T(8,128)(2,1)}, bf16[64,18432]{1,0:T(8,128)(2,1)}, u32[]{:S(2)}, u32[]{:S(2)}) collective-permute-start(bf16[64,18432]{1,0:T(8,128)(2,1)} %get-tuple-element.32.refs_2_.refs_1_), channel_id=1, source_target_pairs={{0,4},{1,5},{2,6},{3,7},{4,0},{5,1},{6,2},{7,3}} | collective-permute-start | bytes 7077896 | tf_op jit(solution)/shard_map/ppermute | solution.py:248
  258.7 356.7 %collective-permute-start.30 = (bf16[128,18432]{1,0:T(8,128)(2,1)}, bf16[128,18432]{1,0:T(8,128)(2,1)}, u32[]{:S(2)}, u32[]{:S(2)}) collective-permute-start(bf16[128,18432]{1,0:T(8,128)(2,1)} %get-tuple-element.44), channel_id=1, source_target_pairs={{0,1},{1,0},{2,3},{3,2},{4,5},{5,4},{6,7},{7,6}} | collective-permute-start | bytes 14155784 | tf_op jit(solution)/shard_map/ppermute | solution.py:248
  258.7 56.5 %collective-permute-start.18 = (bf16[64,18432]{1,0:T(8,128)(2,1)}, bf16[64,18432]{1,0:T(8,128)(2,1)}, u32[]{:S(2)}, u32[]{:S(2)}) collective-permute-start(bf16[64,18432]{1,0:T(8,128)(2,1)} %collective-permute-done.16.refs_0_), channel_id=1, source_target_pairs={{0,1},{1,0},{2,3},{3,2},{4,5},{5,4},{6,7},{7,6}} | collective-permute-start | bytes 7077896 | tf_op jit(solution)/shard_map/ppermute | solution.py:248
  259.2 56.0 %collective-permute-start.19 = (bf16[64,18432]{1,0:T(8,128)(2,1)}, bf16[64,18432]{1,0:T(8,128)(2,1)}, u32[]{:S(2)}, u32[]{:S(2)}) collective-permute-start(bf16[64,18432]{1,0:T(8,128)(2,1)} %collective-permute-done.17.refs_1_), channel_id=1, source_target_pairs={{0,1},{1,0},{2,3},{3,2},{4,5},{5,4},{6,7},{7,6}} | collective-permute-start | bytes 7077896 | tf_op jit(solution)/shard_map/ppermute | solution.py:248
  313.8 56.5 %collective-permute-start.42 = (bf16[64,18432]{1,0:T(8,128)(2,1)}, bf16[64,18432]{1,0:T(8,128)(2,1)}, u32[]{:S(2)}, u32[]{:S(2)}) collective-permute-start(bf16[64,18432]{1,0:T(8,128)(2,1)} %collective-permute-done.31.refs_0_), channel_id=1, source_target_pairs={{0,4},{1,5},{2,6},{3,7},{4,0},{5,1},{6,2},{7,3}} | collective-permute-start | bytes 7077896 | tf_op jit(solution)/shard_map/ppermute | solution.py:248
  314.3 57.2 %collective-permute-start.43 = (bf16[64,18432]{1,0:T(8,128)(2,1)}, bf16[64,18432]{1,0:T(8,128)(2,1)}, u32[]{:S(2)}, u32[]{:S(2)}) collective-permute-start(bf16[64,18432]{1,0:T(8,128)(2,1)} %collective-permute-done.32.refs_1_), channel_id=1, source_target_pairs={{0,2},{1,3},{2,0},{3,1},{4,6},{5,7},{6,4},{7,5}} | collective-permute-start | bytes 7077896 | tf_op jit(solution)/shard_map/ppermute | solution.py:248
  315.2 57.8 %collective-permute-start.12 = (bf16[64,18432]{1,0:T(8,128)(2,1)S(1)}, bf16[64,18432]{1,0:T(8,128)(2,1)}, u32[]{:S(2)}, u32[]{:S(2)}) collective-permute-start(bf16[64,18432]{1,0:T(8,128)(2,1)S(1)} %collective-permute-done.10.refs_0_), channel_id=1, source_target_pairs={{0,1},{1,0},{2,3},{3,2},{4,5},{5,4},{6,7},{7,6}} | collective-permute-start | bytes 7077896 | tf_op jit(solution)/shard_map/ppermute | solution.py:248
  315.3 57.8 %collective-permute-start.13 = (bf16[64,18432]{1,0:T(8,128)(2,1)}, bf16[64,18432]{1,0:T(8,128)(2,1)}, u32[]{:S(2)}, u32[]{:S(2)}) collective-permute-start(bf16[64,18432]{1,0:T(8,128)(2,1)} %collective-permute-done.11.refs_1_), channel_id=1, source_target_pairs={{0,1},{1,0},{2,3},{3,2},{4,5},{5,4},{6,7},{7,6}} | collective-permute-start | bytes 7077896 | tf_op jit(solution)/shard_map/ppermute | solution.py:248
  370.4 57.7 %collective-permute-start.21 = (bf16[64,18432]{1,0:T(8,128)(2,1)S(1)}, bf16[64,18432]{1,0:T(8,128)(2,1)}, u32[]{:S(2)}, u32[]{:S(2)}) collective-permute-start(bf16[64,18432]{1,0:T(8,128)(2,1)S(1)} %collective-permute-done.10.refs_0_), channel_id=1, source_target_pairs={{0,4},{1,5},{2,6},{3,7},{4,0},{5,1},{6,2},{7,3}} | collective-permute-start | bytes 7077896 | tf_op jit(solution)/shard_map/ppermute | solution.py:248
  371.5 56.6 %collective-permute-start.22 = (bf16[64,18432]{1,0:T(8,128)(2,1)}, bf16[64,18432]{1,0:T(8,128)(2,1)}, u32[]{:S(2)}, u32[]{:S(2)}) collective-permute-start(bf16[64,18432]{1,0:T(8,128)(2,1)} %collective-permute-done.11.refs_1_), channel_id=1, source_target_pairs={{0,2},{1,3},{2,0},{3,1},{4,6},{5,7},{6,4},{7,5}} | collective-permute-start | bytes 7077896 | tf_op jit(solution)/shard_map/ppermute | solution.py:248
  373.0 55.6 %collective-permute-start.44 = (bf16[64,18432]{1,0:T(8,128)(2,1)}, bf16[64,18432]{1,0:T(8,128)(2,1)}, u32[]{:S(2)}, u32[]{:S(2)}) collective-permute-start(bf16[64,18432]{1,0:T(8,128)(2,1)} %collective-permute-done.42.refs_0_), channel_id=1, source_target_pairs={{0,1},{1,0},{2,3},{3,2},{4,5},{5,4},{6,7},{7,6}} | collective-permute-start | bytes 7077896 | tf_op jit(solution)/shard_map/ppermute | solution.py:248
  373.0 55.6 %collective-permute-start.45 = (bf16[64,18432]{1,0:T(8,128)(2,1)}, bf16[64,18432]{1,0:T(8,128)(2,1)}, u32[]{:S(2)}, u32[]{:S(2)}) collective-permute-start(bf16[64,18432]{1,0:T(8,128)(2,1)} %collective-permute-done.43.refs_1_), channel_id=1, source_target_pairs={{0,1},{1,0},{2,3},{3,2},{4,5},{5,4},{6,7},{7,6}} | collective-permute-start | bytes 7077896 | tf_op jit(solution)/shard_map/ppermute | solution.py:248
  428.1 133.5 %collective-permute-start.41 = (bf16[128,18432]{1,0:T(8,128)(2,1)}, bf16[128,18432]{1,0:T(8,128)(2,1)}, u32[]{:S(2)}, u32[]{:S(2)}) collective-permute-start(bf16[128,18432]{1,0:T(8,128)(2,1)} %get-tuple-element.48), channel_id=1, source_target_pairs={{0,1},{1,0},{2,3},{3,2},{4,5},{5,4},{6,7},{7,6}} | collective-permute-start | bytes 14155784 | tf_op jit(solution)/shard_map/ppermute | solution.py:248
  428.1 111.8 %collective-permute-start.35 = (bf16[128,18432]{1,0:T(8,128)(2,1)}, bf16[128,18432]{1,0:T(8,128)(2,1)}, u32[]{:S(2)}, u32[]{:S(2)}) collective-permute-start(bf16[128,18432]{1,0:T(8,128)(2,1)} %get-tuple-element.46), channel_id=1, source_target_pairs={{0,1},{1,0},{2,3},{3,2},{4,5},{5,4},{6,7},{7,6}} | collective-permute-start | bytes 14155784 | tf_op jit(solution)/shard_map/ppermute | solution.py:248
  428.6 55.2 %collective-permute-start.23 = (bf16[64,18432]{1,0:T(8,128)(2,1)}, bf16[64,18432]{1,0:T(8,128)(2,1)S(1)}, u32[]{:S(2)}, u32[]{:S(2)}) collective-permute-start(bf16[64,18432]{1,0:T(8,128)(2,1)} %collective-permute-done.21.refs_0_), channel_id=1, source_target_pairs={{0,1},{1,0},{2,3},{3,2},{4,5},{5,4},{6,7},{7,6}} | collective-permute-start | bytes 7077896 | tf_op jit(solution)/shard_map/ppermute | solution.py:248
  428.7 55.2 %collective-permute-start.24 = (bf16[64,18432]{1,0:T(8,128)(2,1)}, bf16[64,18432]{1,0:T(8,128)(2,1)}, u32[]{:S(2)}, u32[]{:S(2)}) collective-permute-start(bf16[64,18432]{1,0:T(8,128)(2,1)} %collective-permute-done.22.refs_1_), channel_id=1, source_target_pairs={{0,1},{1,0},{2,3},{3,2},{4,5},{5,4},{6,7},{7,6}} | collective-permute-start | bytes 7077896 | tf_op jit(solution)/shard_map/ppermute | solution.py:248
  483.8 132.7 %collective-permute-start.20 = (bf16[128,18432]{1,0:T(8,128)(2,1)}, bf16[128,18432]{1,0:T(8,128)(2,1)}, u32[]{:S(2)}, u32[]{:S(2)}) collective-permute-start(bf16[128,18432]{1,0:T(8,128)(2,1)} %get-tuple-element.40), channel_id=1, source_target_pairs={{0,1},{1,0},{2,3},{3,2},{4,5},{5,4},{6,7},{7,6}} | collective-permute-start | bytes 14155784 | tf_op jit(solution)/shard_map/ppermute | solution.py:248
  485.2 61.8 %collective-permute-start.14 = (bf16[128,18432]{1,0:T(8,128)(2,1)}, bf16[128,18432]{1,0:T(8,128)(2,1)}, u32[]{:S(2)}, u32[]{:S(2)}) collective-permute-start(bf16[128,18432]{1,0:T(8,128)(2,1)} %get-tuple-element.38), channel_id=1, source_target_pairs={{0,1},{1,0},{2,3},{3,2},{4,5},{5,4},{6,7},{7,6}} | collective-permute-start | bytes 14155784 | tf_op jit(solution)/shard_map/ppermute | solution.py:248
  556.6 53.8 %collective-permute-start.47 = (bf16[64,18432]{1,0:T(8,128)(2,1)}, bf16[64,18432]{1,0:T(8,128)(2,1)S(1)}, u32[]{:S(2)}, u32[]{:S(2)}) collective-permute-start(bf16[64,18432]{1,0:T(8,128)(2,1)} %get-tuple-element.73), channel_id=1, source_target_pairs={{0,2},{1,3},{2,0},{3,1},{4,6},{5,7},{6,4},{7,5}} | collective-permute-start | bytes 7077896 | tf_op jit(solution)/shard_map/ppermute | solution.py:248
  557.1 53.8 %collective-permute-start.52 = (bf16[64,18432]{1,0:T(8,128)(2,1)}, bf16[64,18432]{1,0:T(8,128)(2,1)S(1)}, u32[]{:S(2)}, u32[]{:S(2)}) collective-permute-start(bf16[64,18432]{1,0:T(8,128)(2,1)} %get-tuple-element.74), channel_id=1, source_target_pairs={{0,4},{1,5},{2,6},{3,7},{4,0},{5,1},{6,2},{7,3}} | collective-permute-start | bytes 7077896 | tf_op jit(solution)/shard_map/ppermute | solution.py:248
  561.5 212.3 %collective-permute-start.9 = (bf16[128,18432]{1,0:T(8,128)(2,1)}, bf16[128,18432]{1,0:T(8,128)(2,1)S(1)}, u32[]{:S(2)}, u32[]{:S(2)}) collective-permute-start(bf16[128,18432]{1,0:T(8,128)(2,1)} %get-tuple-element.36), channel_id=1, source_target_pairs={{0,1},{1,0},{2,3},{3,2},{4,5},{5,4},{6,7},{7,6}} | collective-permute-start | bytes 14155784 | tf_op jit(solution)/shard_map/ppermute | solution.py:248
  610.5 54.3 %collective-permute-start.26 = (bf16[64,18432]{1,0:T(8,128)(2,1)}, bf16[64,18432]{1,0:T(8,128)(2,1)S(1)}, u32[]{:S(2)}, u32[]{:S(2)}) collective-permute-start(bf16[64,18432]{1,0:T(8,128)(2,1)} %get-tuple-element.65), channel_id=1, source_target_pairs={{0,2},{1,3},{2,0},{3,1},{4,6},{5,7},{6,4},{7,5}} | collective-permute-start | bytes 7077896 | tf_op jit(solution)/shard_map/ppermute | solution.py:248
  611.0 54.3 %collective-permute-start.49 = (bf16[64,18432]{1,0:T(8,128)(2,1)}, bf16[64,18432]{1,0:T(8,128)(2,1)S(1)}, u32[]{:S(2)}, u32[]{:S(2)}) collective-permute-start(bf16[64,18432]{1,0:T(8,128)(2,1)} %get-tuple-element.66), channel_id=1, source_target_pairs={{0,4},{1,5},{2,6},{3,7},{4,0},{5,1},{6,2},{7,3}} | collective-permute-start | bytes 7077896 | tf_op jit(solution)/shard_map/ppermute | solution.py:248
  615.4 99.9 %collective-permute-start.36 = (bf16[64,18432]{1,0:T(8,128)(2,1)}, bf16[64,18432]{1,0:T(8,128)(2,1)S(1)}, u32[]{:S(2)}, u32[]{:S(2)}) collective-permute-start(bf16[64,18432]{1,0:T(8,128)(2,1)} %get-tuple-element.69), channel_id=1, source_target_pairs={{0,2},{1,3},{2,0},{3,1},{4,6},{5,7},{6,4},{7,5}} | collective-permute-start | bytes 7077896 | tf_op jit(solution)/shard_map/ppermute | solution.py:248
  616.5 99.3 %collective-permute-start.54 = (bf16[64,18432]{1,0:T(8,128)(2,1)}, bf16[64,18432]{1,0:T(8,128)(2,1)S(1)}, u32[]{:S(2)}, u32[]{:S(2)}) collective-permute-start(bf16[64,18432]{1,0:T(8,128)(2,1)} %get-tuple-element.70), channel_id=1, source_target_pairs={{0,4},{1,5},{2,6},{3,7},{4,0},{5,1},{6,2},{7,3}} | collective-permute-start | bytes 7077896 | tf_op jit(solution)/shard_map/ppermute | solution.py:248
  664.8 101.6 %collective-permute-start.48 = (bf16[64,18432]{1,0:T(8,128)(2,1)S(1)}, bf16[64,18432]{1,0:T(8,128)(2,1)S(1)}, u32[]{:S(2)}, u32[]{:S(2)}) collective-permute-start(bf16[64,18432]{1,0:T(8,128)(2,1)S(1)} %get-tuple-element.71), channel_id=1, source_target_pairs={{0,4},{1,5},{2,6},{3,7},{4,0},{5,1},{6,2},{7,3}} | collective-permute-start | bytes 7077896 | tf_op jit(solution)/shard_map/ppermute | solution.py:248
  666.7 100.6 %collective-permute-start.53 = (bf16[64,18432]{1,0:T(8,128)(2,1)S(1)}, bf16[64,18432]{1,0:T(8,128)(2,1)S(1)}, u32[]{:S(2)}, u32[]{:S(2)}) collective-permute-start(bf16[64,18432]{1,0:T(8,128)(2,1)S(1)} %get-tuple-element.72), channel_id=1, source_target_pairs={{0,2},{1,3},{2,0},{3,1},{4,6},{5,7},{6,4},{7,5}} | collective-permute-start | bytes 7077896 | tf_op jit(solution)/shard_map/ppermute | solution.py:248
  715.3 101.1 %collective-permute-start.15 = (bf16[64,18432]{1,0:T(8,128)(2,1)}, bf16[64,18432]{1,0:T(8,128)(2,1)S(1)}, u32[]{:S(2)}, u32[]{:S(2)}) collective-permute-start(bf16[64,18432]{1,0:T(8,128)(2,1)} %get-tuple-element.61), channel_id=1, source_target_pairs={{0,2},{1,3},{2,0},{3,1},{4,6},{5,7},{6,4},{7,5}} | collective-permute-start | bytes 7077896 | tf_op jit(solution)/shard_map/ppermute | solution.py:248
  715.9 101.2 %collective-permute-start.51 = (bf16[64,18432]{1,0:T(8,128)(2,1)}, bf16[64,18432]{1,0:T(8,128)(2,1)}, u32[]{:S(2)}, u32[]{:S(2)}) collective-permute-start(bf16[64,18432]{1,0:T(8,128)(2,1)} %get-tuple-element.62), channel_id=1, source_target_pairs={{0,4},{1,5},{2,6},{3,7},{4,0},{5,1},{6,2},{7,3}} | collective-permute-start | bytes 7077896 | tf_op jit(solution)/shard_map/ppermute | solution.py:248
  766.4 99.6 %collective-permute-start.27 = (bf16[64,18432]{1,0:T(8,128)(2,1)}, bf16[64,18432]{1,0:T(8,128)(2,1)}, u32[]{:S(2)}, u32[]{:S(2)}) collective-permute-start(bf16[64,18432]{1,0:T(8,128)(2,1)} %get-tuple-element.63), channel_id=1, source_target_pairs={{0,4},{1,5},{2,6},{3,7},{4,0},{5,1},{6,2},{7,3}} | collective-permute-start | bytes 7077896 | tf_op jit(solution)/shard_map/ppermute | solution.py:248
  767.3 98.7 %collective-permute-start.50 = (bf16[64,18432]{1,0:T(8,128)(2,1)S(1)}, bf16[64,18432]{1,0:T(8,128)(2,1)}, u32[]{:S(2)}, u32[]{:S(2)}) collective-permute-start(bf16[64,18432]{1,0:T(8,128)(2,1)S(1)} %get-tuple-element.64), channel_id=1, source_target_pairs={{0,2},{1,3},{2,0},{3,1},{4,6},{5,7},{6,4},{7,5}} | collective-permute-start | bytes 7077896 | tf_op jit(solution)/shard_map/ppermute | solution.py:248
  (30 other events, 861.3 us)
